TPU v7x, 32 devices: a whole 2x2x4 slice. The times are simulated.
32 devices in a mesh: seq: 8 (over y, x, core), dp: 4 (over z).
Axes of the slice: x: 2, y: 2, z: 4, core: 2. Of those that a mesh axis runs over, the one named last changes fastest.
Arguments:
- queries: bfloat16 [8, 512, 4096], P('dp', 'seq'), may hold values from -8 to 8
- unrotated_key_rows: bfloat16 [8, 512, 1024], P('dp', 'seq'), may hold values from -8 to 8
- value_projection_rows: bfloat16 [8, 512, 1024], P('dp', 'seq'), may hold values from -6 to 6
- attention_output_gradient: bfloat16 [8, 512, 4096], P('dp', 'seq'), may hold values from -16 to 16
- normed_hidden_input: bfloat16 [8, 512, 4096], P('dp', 'seq'), may hold values from -6 to 6
- adapter_down_weight: bfloat16 [4096, 64], replicated, may hold values from -0.01171875 to 0.01171875
- adapter_up_weight: bfloat16 [64, 4096], replicated, may hold values from -0.01171875 to 0.01171875
- lengths: int32 [8], P('dp'), may hold values from 256 to 512, as said below
- offsets: int32 [8], P('dp'), may hold values from 0 to 31
Outputs:
- grad_query: bfloat16 [8, 512, 4096], P('dp', 'seq')
- grad_key: bfloat16 [8, 512, 1024], P('dp', 'seq')
- grad_value: bfloat16 [8, 512, 1024], P('dp', 'seq')
- grad_down: float32 [4096, 64], P('seq')
- grad_up: float32 [64, 4096], P(None, 'seq')
Inputs may be any that keep to these rules, and one draw needn't show every extreme that they name: `lengths`: in every draw at least one rollout has all 512 positions valid.
All inputs are finite; a program needn't handle non-finite values.
Results may differ from a plain program's by a relative error of at most 0.018.
The roundings to bfloat16 on the way count: a program that leaves them out, or rounds other values in their place, can miss the bound.
Values may be sent and summed in bfloat16 or wider, within the bound.
A program may use at most 64 MiB of HBM per device.

v0:
```python
from functools import partial

import jax
import jax.numpy as jnp
from jax import lax
from jax.sharding import PartitionSpec as P

HEAD_WIDTH = 128


rotary_base = 500000.0


def partner_2(value, axis, distance):
    mask = 2**distance
    pairs = [(source, source ^ mask) for source in range(lax.axis_size(axis))]
    return lax.ppermute(value, axis, pairs)


def rotary_tables(length, head_size):
    half_size = head_size // 2
    frequency = rotary_base ** (-(jnp.arange(half_size, dtype=jnp.float32) * 2.0 / head_size))
    angles = jnp.arange(length, dtype=jnp.float32)[:, None] * frequency[None, :]
    return (jnp.cos(angles), jnp.sin(angles))


def rotate(fields, cosine, sine_table, direction):
    half_size = fields.shape[-1] // 2
    first_half = fields[..., :half_size]
    second_half = fields[..., half_size:]
    cos_wide = cosine[:, None, :]
    sin_wide = direction * sine_table[:, None, :]
    return jnp.concatenate(
        [
            first_half * cos_wide - second_half * sin_wide,
            second_half * cos_wide + first_half * sin_wide,
        ],
        axis=-1,
    )


def contract_axes(first_operand, second_operand, first_axis, second_axis):
    return lax.dot_general(
        first_operand,
        second_operand,
        (((first_axis,), (second_axis,)), ((), ())),
        preferred_element_type=jnp.float32,
    )


def block_terms(rot_query, rot_key, value_head, grad_head, offset, begin_row, end_row, score_scale):
    row_index = jnp.arange(begin_row, end_row, dtype=jnp.int32)[:, None]
    col_index = jnp.arange(end_row, dtype=jnp.int32)[None, :]
    visible = (col_index == row_index) | (col_index >= offset) & (col_index <= row_index)
    query_block = rot_query[begin_row:end_row]
    grad_block = grad_head[begin_row:end_row]
    key_block = rot_key[:end_row]
    value_block = value_head[:end_row]
    scores = contract_axes(query_block, key_block, 1, 1) * score_scale
    row_max = jnp.max(jnp.where(visible, scores, -jnp.inf), axis=1, keepdims=True)
    row_total = jnp.sum(jnp.where(visible, jnp.exp(scores - row_max), 0.0), axis=1, keepdims=True)
    grad_prob = contract_axes(grad_block, value_block, 1, 1)
    probability = jnp.where(visible, jnp.exp(scores - row_max), 0.0) / row_total
    row_delta = jnp.sum(probability * grad_prob, axis=1, keepdims=True)
    prob_low = probability.astype(jnp.bfloat16)
    grad_score = (probability * (grad_prob - row_delta) * score_scale).astype(jnp.bfloat16)
    block_grad = jnp.dot(grad_score, key_block, preferred_element_type=jnp.float32)
    key_add = contract_axes(grad_score, query_block, 0, 0)
    value_add = contract_axes(prob_low, grad_block, 0, 0)
    return (block_grad, key_add, value_add)


def head_backward(rot_query, rot_key, value_head, grad_head, offset, block_rows):
    length = rot_query.shape[0]
    head_size = rot_query.shape[1]
    score_scale = head_size ** (-0.5)
    query_parts = []
    key_terms = []
    value_terms = []
    for block_index in range(length // block_rows):
        begin_row = block_index * block_rows
        end_row = begin_row + block_rows
        live_terms = partial(
            block_terms,
            rot_query,
            rot_key,
            value_head,
            grad_head,
            offset,
            begin_row,
            end_row,
            score_scale,
        )
        results = live_terms()
        block_grad, key_add, value_add = results
        query_parts.append(block_grad)
        key_terms.append(jnp.pad(key_add, ((0, length - end_row), (0, 0))))
        value_terms.append(jnp.pad(value_add, ((0, length - end_row), (0, 0))))
    key_accum = key_terms[0]
    value_accum = value_terms[0]
    for term_index in range(1, len(key_terms)):
        key_accum = key_accum + key_terms[term_index]
        value_accum = value_accum + value_terms[term_index]
    return (jnp.concatenate(query_parts, axis=0), key_accum, value_accum)


def arrange_rows(rows, share, part_rows, key_groups):
    rollout_count = rows.shape[0]
    split = rows.reshape(rollout_count, share, part_rows, key_groups, HEAD_WIDTH)
    return jnp.transpose(split, (0, 2, 3, 1, 4)).reshape(
        rollout_count, part_rows, key_groups * share, HEAD_WIDTH
    )


def join_group(paired, share, seq_parts, part_rows):
    my_index = lax.axis_index("seq")
    rollout_count = paired.shape[1]
    local_keys = paired.shape[3]
    joined = paired[None]
    for bit in range(share.bit_length() - 1):
        partner = partner_2(joined, "seq", bit)
        upper = my_index // (1 << bit) % 2
        joined = jnp.where(
            upper == 0,
            jnp.concatenate([joined, partner], axis=0),
            jnp.concatenate([partner, joined], axis=0),
        )
    ordered = joined.reshape(share, 2, rollout_count, seq_parts, part_rows, local_keys, HEAD_WIDTH)
    ordered = jnp.transpose(ordered, (1, 2, 3, 0, 4, 5, 6))
    return ordered.reshape(2, rollout_count, seq_parts * share * part_rows, local_keys, HEAD_WIDTH)


def reduce_group(partial_sums, share, seq_parts, part_rows):
    my_index = lax.axis_index("seq")
    rollout_count = partial_sums.shape[1]
    local_keys = partial_sums.shape[3]
    split = partial_sums.reshape(
        2, rollout_count, seq_parts, share, part_rows, local_keys, HEAD_WIDTH
    )
    split = jnp.transpose(split, (3, 0, 1, 2, 4, 5, 6))
    for bit in reversed(range(share.bit_length() - 1)):
        half = split.shape[0] // 2
        lower_half = split[:half]
        upper_half = split[half:]
        upper = my_index // (1 << bit) % 2
        keep = jnp.where(upper == 0, lower_half, upper_half)
        outgoing = jnp.where(upper == 0, upper_half, lower_half)
        split = keep + partner_2(outgoing.astype(jnp.bfloat16), "seq", bit).astype(outgoing.dtype)
    return split[0].reshape(2, rollout_count, seq_parts * part_rows, local_keys, HEAD_WIDTH)


def on_device(
    queries,
    unrotated_key_rows,
    value_projection_rows,
    attention_output_gradient,
    normed_hidden_input,
    adapter_down_weight,
    adapter_up_weight,
    lengths,
    offsets,
):
    rollout_count = queries.shape[0]
    tokens = queries.shape[1]
    seq_parts = lax.axis_size("seq")
    length = tokens * seq_parts
    query_width = queries.shape[2]
    head_count = query_width // HEAD_WIDTH
    key_groups = unrotated_key_rows.shape[2] // HEAD_WIDTH
    local_heads = head_count // seq_parts
    adapter_rank_size = adapter_down_weight.shape[1]
    share = max(1, seq_parts // key_groups)
    part_rows = tokens // share
    query_tokens = queries.reshape(rollout_count, tokens, head_count, HEAD_WIDTH)
    grad_tokens = attention_output_gradient.reshape(rollout_count, tokens, head_count, HEAD_WIDTH)
    key_arranged = arrange_rows(unrotated_key_rows, share, part_rows, key_groups)
    value_arranged = arrange_rows(value_projection_rows, share, part_rows, key_groups)
    query_heads, key_parted, value_parted, grad_heads = (
        lax.all_to_all(query_tokens, "seq", split_axis=2, concat_axis=1, tiled=True),
        lax.all_to_all(key_arranged, "seq", split_axis=2, concat_axis=1, tiled=True),
        lax.all_to_all(value_arranged, "seq", split_axis=2, concat_axis=1, tiled=True),
        lax.all_to_all(grad_tokens, "seq", split_axis=2, concat_axis=1, tiled=True),
    )
    paired = join_group(jnp.stack([key_parted, value_parted], axis=0), share, seq_parts, part_rows)
    key_heads = paired[0]
    value_heads = paired[1]
    local_keys = key_heads.shape[2]
    cosine, sine_table = rotary_tables(length, HEAD_WIDTH)
    positions = jnp.arange(length, dtype=jnp.int32)
    keep_mask = (positions[None, :] >= offsets[:, None]) & (positions[None, :] < lengths[:, None])
    grad_heads = jnp.where(keep_mask[:, :, None, None], grad_heads, jnp.zeros_like(grad_heads))
    rot_query = rotate(query_heads.astype(jnp.float32), cosine, sine_table, 1.0).astype(
        jnp.bfloat16
    )
    rot_key = rotate(key_heads.astype(jnp.float32), cosine, sine_table, 1.0).astype(jnp.bfloat16)
    block_rows = min(512, length)
    query_rolls = []
    key_rolls = []
    value_rolls = []
    for rollout_slot in range(rollout_count):
        query_list = []
        key_list = []
        value_list = []
        for head_slot in range(local_heads):
            key_slot = head_slot * local_keys // local_heads
            query_grad, key_grad, value_grad = head_backward(
                rot_query[rollout_slot, :, head_slot],
                rot_key[rollout_slot, :, key_slot],
                value_heads[rollout_slot, :, key_slot],
                grad_heads[rollout_slot, :, head_slot],
                offsets[rollout_slot],
                block_rows,
            )
            query_list.append(
                rotate(query_grad[:, None, :], cosine, sine_table, -1.0)[:, 0].astype(jnp.bfloat16)
            )
            key_list.append(
                rotate(key_grad[:, None, :], cosine, sine_table, -1.0)[:, 0].astype(jnp.bfloat16)
            )
            value_list.append(value_grad.astype(jnp.bfloat16))
        query_rolls.append(jnp.stack(query_list, axis=1))
        key_rolls.append(jnp.stack(key_list, axis=1))
        value_rolls.append(jnp.stack(value_list, axis=1))
    query_back = jnp.stack(query_rolls, axis=0)
    key_parts = jnp.stack(key_rolls, axis=0)
    value_parts = jnp.stack(value_rolls, axis=0)
    shared_heads = local_heads // local_keys
    key_local = (
        key_parts.astype(jnp.float32)
        .reshape(rollout_count, length, local_keys, shared_heads, HEAD_WIDTH)
        .sum(axis=3)
    )
    value_local = (
        value_parts.astype(jnp.float32)
        .reshape(rollout_count, length, local_keys, shared_heads, HEAD_WIDTH)
        .sum(axis=3)
    )
    summed = reduce_group(
        jnp.stack([key_local, value_local], axis=0), share, seq_parts, part_rows
    ).astype(jnp.bfloat16)
    query_result, key_result, value_result = (
        lax.all_to_all(query_back, "seq", split_axis=1, concat_axis=2, tiled=True),
        lax.all_to_all(summed[0], "seq", split_axis=1, concat_axis=2, tiled=True),
        lax.all_to_all(summed[1], "seq", split_axis=1, concat_axis=2, tiled=True),
    )
    key_total = jnp.transpose(
        key_result.reshape(rollout_count, part_rows, key_groups, share, HEAD_WIDTH), (0, 3, 1, 2, 4)
    ).reshape(rollout_count, tokens, key_groups * HEAD_WIDTH)
    value_total = jnp.transpose(
        value_result.reshape(rollout_count, part_rows, key_groups, share, HEAD_WIDTH),
        (0, 3, 1, 2, 4),
    ).reshape(rollout_count, tokens, key_groups * HEAD_WIDTH)
    flattened_query = query_result.reshape(rollout_count * tokens, query_width)
    hidden_state = normed_hidden_input.reshape(rollout_count * tokens, normed_hidden_input.shape[2])
    adapter_latent = jnp.dot(
        hidden_state, adapter_down_weight, preferred_element_type=jnp.float32
    ).astype(jnp.bfloat16)
    backward_gradient = contract_axes(flattened_query, adapter_up_weight, 1, 1).astype(jnp.bfloat16)
    joined_terms = lax.psum_scatter(
        jnp.concatenate(
            [
                contract_axes(hidden_state, backward_gradient, 0, 0),
                contract_axes(flattened_query, adapter_latent, 0, 0),
            ],
            axis=1,
        ).astype(jnp.bfloat16),
        "seq",
        scatter_dimension=0,
        tiled=True,
    ).astype(jnp.float32)
    down_local = joined_terms[:, :adapter_rank_size]
    up_local = joined_terms[:, adapter_rank_size:]
    down_sum, up_sum = (
        lax.psum(down_local.astype(jnp.bfloat16), "dp").astype(jnp.float32),
        lax.psum(up_local.astype(jnp.bfloat16), "dp").astype(jnp.float32),
    )
    return (
        flattened_query.reshape(rollout_count, tokens, query_width),
        key_total,
        value_total,
        down_sum,
        up_sum.T,
    )


def solution(mesh):
    in_specs = (
        P("dp", "seq", None),
        P("dp", "seq", None),
        P("dp", "seq", None),
        P("dp", "seq", None),
        P("dp", "seq", None),
        P(),
        P(),
        P("dp"),
        P("dp"),
    )
    out_specs = (
        P("dp", "seq", None),
        P("dp", "seq", None),
        P("dp", "seq", None),
        P("seq", None),
        P(None, "seq"),
    )
    return jax.shard_map(
        on_device, mesh=mesh, in_specs=in_specs, out_specs=out_specs, check_vma=False
    )
```

profile of v0, /device:TPU:0, one launch (start us, length us, event | category | flops | bytes accessed | tf_op | source)
XLA Modules:
  0.0 218.1 jit_solution(3533386464252049813)
XLA Ops:
  7.2 1.9 copy_bitcast_fusion.3
  9.1 5.2 %all-to-all-start.1 = ((bf16[2,64,8,128]{3,1,0,2:T(8,128)(2,1)}), bf16[2,64,8,128]{3,1,0,2:T(8,128)(2,1)S(1)}, u32[]{:S(2)}, u32[]{:S(2)}) async-start(bf16[2,64,8,128]{3,1,0,2:T(8,128)(2,1)} %copy_bitcast_fusion.3), calls=%async_computation.1 | async-start | bytes 524288 | tf_op jit(solution)/shard_map/all_to_all | solution.py:180
  14.3 1.3 fusion.96
  15.6 1.0 fusion.38
  16.6 1.3 copy_bitcast_fusion.1
  17.9 1.3 copy_bitcast_fusion
  19.2 0.8 copy_bitcast_fusion.2
  20.0 1.2 all-to-all-done.1
  21.2 3.4 %all-to-all-start.3 = ((bf16[2,64,8,128]{3,1,0,2:T(8,128)(2,1)}), bf16[2,64,8,128]{3,1,0,2:T(8,128)(2,1)S(1)}, u32[]{:S(2)}, u32[]{:S(2)}) async-start(bf16[2,64,8,128]{3,1,0,2:T(8,128)(2,1)} %copy_bitcast_fusion.2), calls=%async_computation.3 | async-start | bytes 524288 | tf_op jit(solution)/shard_map/all_to_all | solution.py:181
  24.6 0.7 iota_compare_fusion.3
  25.3 6.1 %all-to-all-done.3 = bf16[2,64,8,128]{3,1,0,2:T(8,128)(2,1)S(1)} async-done(((bf16[2,64,8,128]{3,1,0,2:T(8,128)(2,1)}), bf16[2,64,8,128]{3,1,0,2:T(8,128)(2,1)S(1)}, u32[]{:S(2)}, u32[]{:S(2)}) %all-to-all-start.3) | async-done | bytes 262176 | tf_op jit(solution)/shard_map/all_to_all | solution.py:181
  31.4 3.6 %all-to-all-start = ((bf16[2,64,32,128]{3,1,0,2:T(8,128)(2,1)}), bf16[2,64,32,128]{3,1,0,2:T(8,128)(2,1)S(1)}, u32[]{:S(2)}, u32[]{:S(2)}) async-start(bf16[2,64,32,128]{3,1,0,2:T(8,128)(2,1)} %copy_bitcast_fusion.1), calls=%async_computation | async-start | bytes 2097152 | tf_op jit(solution)/shard_map/all_to_all | solution.py:179
  36.2 0.7 fusion.95
  36.9 13.4 %all-to-all-done = bf16[2,64,32,128]{3,1,0,2:T(8,128)(2,1)S(1)} async-done(((bf16[2,64,32,128]{3,1,0,2:T(8,128)(2,1)}), bf16[2,64,32,128]{3,1,0,2:T(8,128)(2,1)S(1)}, u32[]{:S(2)}, u32[]{:S(2)}) %all-to-all-start) | async-done | bytes 1048608 | tf_op jit(solution)/shard_map/all_to_all | solution.py:179
  50.3 4.4 %all-to-all-start.2 = ((bf16[2,64,32,128]{3,1,0,2:T(8,128)(2,1)}), bf16[2,64,32,128]{3,1,0,2:T(8,128)(2,1)}, u32[]{:S(2)}, u32[]{:S(2)}) async-start(bf16[2,64,32,128]{3,1,0,2:T(8,128)(2,1)} %copy_bitcast_fusion), calls=%async_computation.2 | async-start | bytes 2097152 | tf_op jit(solution)/shard_map/all_to_all | solution.py:182
  55.2 0.8 copy-done.25
  56.1 0.8 add_convert_fusion
  56.9 1.3 convolution_multiply_fusion.6
  58.2 1.3 convolution_multiply_fusion.5
  59.6 1.4 convolution_multiply_fusion.4
  61.1 1.3 convolution_multiply_fusion.2
  62.4 1.4 convolution_multiply_fusion.1
  63.8 1.3 convolution_multiply_fusion
  65.1 4.9 %all-to-all-done.2 = bf16[2,64,32,128]{3,1,0,2:T(8,128)(2,1)} async-done(((bf16[2,64,32,128]{3,1,0,2:T(8,128)(2,1)}), bf16[2,64,32,128]{3,1,0,2:T(8,128)(2,1)}, u32[]{:S(2)}, u32[]{:S(2)}) %all-to-all-start.2) | async-done | bytes 1048608 | tf_op jit(solution)/shard_map/all_to_all | solution.py:182
  69.9 1.3 copy.65
  73.1 1.0 fusion.1
  74.8 1.0 fusion.5
  77.5 1.0 fusion.6
  79.2 1.0 fusion.7
  80.2 1.0 fusion.8
  81.8 0.9 multiply_convert_fusion.3
  87.2 0.8 multiply_reduce_fusion.5
  88.0 0.9 multiply_convert_fusion.7
  90.5 0.7 subtract_convert_fusion.17
  91.1 0.7 subtract_convert_fusion.16
  91.9 1.1 pad_maximum_fusion
  93.0 2.4 %copy.68 = bf16[2,512,4,128]{3,2,0,1:T(4,128)(2,1)} copy(bf16[2,512,4,128]{1,3,2,0:T(8,128)(2,1)} %pad_maximum_fusion) | data formatting | bytes 2097152 | tf_op jit(solution)/shard_map/stack | solution.py:224
  95.4 4.2 %all-to-all-start.4 = ((bf16[2,512,4,128]{3,2,0,1:T(4,128)(2,1)}), bf16[2,512,4,128]{3,2,0,1:T(4,128)(2,1)}, u32[]{:S(2)}, u32[]{:S(2)}) async-start(bf16[2,512,4,128]{3,2,0,1:T(4,128)(2,1)} %copy.68), calls=%async_computation.4 | async-start | bytes 2097152 | tf_op jit(solution)/shard_map/all_to_all | solution.py:242
  99.7 1.7 fusion.3
  101.5 1.4 fusion.4
  103.2 1.0 copy.74
  104.2 1.1 convolution_bitcast_fusion.3
  105.3 1.1 convolution_bitcast_fusion.2
  106.3 8.7 %all-to-all-done.4 = bf16[2,512,4,128]{3,2,0,1:T(4,128)(2,1)} async-done(((bf16[2,512,4,128]{3,2,0,1:T(4,128)(2,1)}), bf16[2,512,4,128]{3,2,0,1:T(4,128)(2,1)}, u32[]{:S(2)}, u32[]{:S(2)}) %all-to-all-start.4) | async-done | bytes 1048608 | tf_op jit(solution)/shard_map/all_to_all | solution.py:242
  115.1 3.4 %all-to-all-start.6 = ((bf16[2,512,1,128]{3,0,2,1:T(2,128)(2,1)}), bf16[2,512,1,128]{3,0,2,1:T(2,128)(2,1)S(1)}, u32[]{:S(2)}, u32[]{:S(2)}) async-start(bf16[2,512,1,128]{3,0,2,1:T(2,128)(2,1)} %copy.74), calls=%async_computation.6 | async-start | bytes 524288 | tf_op jit(solution)/shard_map/all_to_all | solution.py:244
  118.5 1.4 copy.69
  119.9 1.8 copy.70
  121.7 2.6 %reshape.691 = bf16[128,4096]{1,0:T(8,128)(2,1)} reshape(bf16[2,64,8,4,128]{4,3,2,1,0:T(4,128)(2,1)} %copy.70) | data formatting | bytes 2097152 | tf_op jit(solution)/shard_map/reshape | solution.py:253
  124.3 3.2 %convolution_convert_fusion = bf16[4096,64]{0,1:T(8,128)(2,1)} fusion(bf16[128,4096]{1,0:T(8,128)(2,1)} %reshape.691, bf16[128,4096]{1,0:T(8,128)(2,1)S(1)} %bitcast.267, bf16[4096,64]{0,1:T(8,128)(2,1)} %param.14), kind=kOutput, calls=%fused_computation | convolution fusion | flops 134488064 | bytes 3145728 | tf_op jit(solution)/shard_map/dot_general | solution.py:43
  127.4 3.1 %fusion = bf16[4096,64]{0,1:T(8,128)(2,1)} fusion(bf16[128,4096]{1,0:T(8,128)(2,1)S(1)} %bitcast.266, bf16[128,4096]{1,0:T(8,128)(2,1)} %reshape.691, bf16[64,4096]{1,0:T(8,128)(2,1)} %param.15), kind=kOutput, calls=%fused_computation.2 | convolution fusion | flops 134488064 | bytes 3145728 | tf_op jit(solution)/shard_map/dot_general | solution.py:43
  130.5 2.3 %pad_maximum_fusion.1 = bf16[4096,128]{0,1:T(8,128)(2,1)} fusion(bf16[4096,64]{0,1:T(8,128)(2,1)} %convolution_convert_fusion, bf16[4096,64]{0,1:T(8,128)(2,1)} %fusion), kind=kLoop, calls=%fused_computation.53 | loop fusion | flops 2097152 | bytes 2097152 | tf_op jit(solution)/shard_map/concatenate | solution.py:260
  132.8 1.5 convolution_bitcast_fusion.1
  138.8 0.7 subtract_convert_fusion.9
  139.5 0.7 subtract_convert_fusion.8
  140.6 0.9 copy.71
  141.5 4.2 %all-to-all-start.5 = ((bf16[2,512,1,128]{3,0,2,1:T(2,128)(2,1)}), bf16[2,512,1,128]{3,0,2,1:T(2,128)(2,1)S(1)}, u32[]{:S(2)}, u32[]{:S(2)}) async-start(bf16[2,512,1,128]{3,0,2,1:T(2,128)(2,1)} %copy.71), calls=%async_computation.5 | async-start | bytes 524288 | tf_op jit(solution)/shard_map/all_to_all | solution.py:243
  145.7 24.8 %reduce-scatter.2.cloned.1.call-done = bf16[512,128]{0,1:T(8,128)(2,1)} async-done(((bf16[4096,128]{0,1:T(8,128)(2,1)}), bf16[512,128]{0,1:T(8,128)(2,1)}) %reduce-scatter.2.cloned.1.call-update) | async-done | bytes 131088 | tf_op jit(solution)/shard_map/reduce_scatter | solution.py:259
  170.5 1.5 slice_bitcast_fusion.24
  172.3 0.8 reshape_transpose_reshape.15
  173.4 0.8 reshape_transpose_reshape.14
  174.2 1.6 reshape_reshape.3
  175.8 32.4 %all-reduce.3.cloned.1.call-done = (bf16[512,64]{0,1:T(8,128)(2,1)}, bf16[64,512]{1,0:T(8,128)(2,1)}) async-done(((bf16[512,64]{0,1:T(8,128)(2,1)}, bf16[64,512]{1,0:T(8,128)(2,1)}), (bf16[512,64]{0,1:T(8,128)(2,1)}, bf16[64,512]{1,0:T(8,128)(2,1)})) %all-reduce.3.cloned.1.call-update) | async-done | bytes 131088 | tf_op jit(solution)/shard_map/psum | solution.py:274
  208.2 1.5 convert_element_type.321
  209.7 1.5 transpose.52
  (149 shorter events, 18.8 us)
Async XLA Ops:
  7.2 117.1 %copy-start = (bf16[2,64,4096]{2,1,0:T(8,128)(2,1)S(1)}, bf16[2,64,4096]{2,1,0:T(8,128)(2,1)}, u32[]{:S(2)}) copy-start(bf16[2,64,4096]{2,1,0:T(8,128)(2,1)} %param.13) | copy-start | bytes 3145732
  7.2 9.4 %copy-start.29 = (bf16[2,64,4096]{2,1,0:T(8,128)(2,1)S(1)}, bf16[2,64,4096]{2,1,0:T(8,128)(2,1)}, u32[]{:S(2)}) copy-start(bf16[2,64,4096]{2,1,0:T(8,128)(2,1)} %param.9) | copy-start | bytes 3145732
  9.1 12.1 %all-to-all-start.1 = ((bf16[2,64,8,128]{3,1,0,2:T(8,128)(2,1)}), bf16[2,64,8,128]{3,1,0,2:T(8,128)(2,1)S(1)}, u32[]{:S(2)}, u32[]{:S(2)}) async-start(bf16[2,64,8,128]{3,1,0,2:T(8,128)(2,1)} %copy_bitcast_fusion.3), calls=%async_computation.1 | async-start | bytes 524288 | tf_op jit(solution)/shard_map/all_to_all | solution.py:180
  14.3 3.7 %copy-start.30 = (bf16[2,64,4096]{2,1,0:T(8,128)(2,1)S(1)}, bf16[2,64,4096]{2,1,0:T(8,128)(2,1)}, u32[]{:S(2)}) copy-start(bf16[2,64,4096]{2,1,0:T(8,128)(2,1)} %param.12) | copy-start | bytes 3145732
  16.6 19.1 %copy-start.24 = (f32[512,64]{1,0:T(8,128)}, f32[512,64]{1,0:T(8,128)S(1)}, u32[]{:S(2)}) copy-start(f32[512,64]{1,0:T(8,128)S(1)} %get-tuple-element.99) | copy-start | bytes 393220
  16.6 19.1 %copy-start.26 = (f32[512,64]{1,0:T(8,128)}, f32[512,64]{1,0:T(8,128)S(1)}, u32[]{:S(2)}) copy-start(f32[512,64]{1,0:T(8,128)S(1)} %get-tuple-element.100) | copy-start | bytes 393220
  16.6 2.6 %copy-start.35 = (bf16[2,64,1024]{2,1,0:T(8,128)(2,1)S(1)}, bf16[2,64,1024]{2,1,0:T(8,128)(2,1)}, u32[]{:S(2)}) copy-start(bf16[2,64,1024]{2,1,0:T(8,128)(2,1)} %param.11) | copy-start | bytes 786436
  17.9 7.3 %copy-start.41 = (s32[2]{0:T(128)S(1)}, s32[2]{0:T(128)}, u32[]{:S(2)}) copy-start(s32[2]{0:T(128)} %param.17) | copy-start | bytes 28
  17.9 7.3 %copy-start.46 = (s32[2]{0:T(128)S(1)}, s32[2]{0:T(128)}, u32[]{:S(2)}) copy-start(s32[2]{0:T(128)} %param.16) | copy-start | bytes 28
  21.2 10.3 %all-to-all-start.3 = ((bf16[2,64,8,128]{3,1,0,2:T(8,128)(2,1)}), bf16[2,64,8,128]{3,1,0,2:T(8,128)(2,1)S(1)}, u32[]{:S(2)}, u32[]{:S(2)}) async-start(bf16[2,64,8,128]{3,1,0,2:T(8,128)(2,1)} %copy_bitcast_fusion.2), calls=%async_computation.3 | async-start | bytes 524288 | tf_op jit(solution)/shard_map/all_to_all | solution.py:181
  31.4 18.9 %all-to-all-start = ((bf16[2,64,32,128]{3,1,0,2:T(8,128)(2,1)}), bf16[2,64,32,128]{3,1,0,2:T(8,128)(2,1)S(1)}, u32[]{:S(2)}, u32[]{:S(2)}) async-start(bf16[2,64,32,128]{3,1,0,2:T(8,128)(2,1)} %copy_bitcast_fusion.1), calls=%async_computation | async-start | bytes 2097152 | tf_op jit(solution)/shard_map/all_to_all | solution.py:179
  50.3 19.6 %all-to-all-start.2 = ((bf16[2,64,32,128]{3,1,0,2:T(8,128)(2,1)}), bf16[2,64,32,128]{3,1,0,2:T(8,128)(2,1)}, u32[]{:S(2)}, u32[]{:S(2)}) async-start(bf16[2,64,32,128]{3,1,0,2:T(8,128)(2,1)} %copy_bitcast_fusion), calls=%async_computation.2 | async-start | bytes 2097152 | tf_op jit(solution)/shard_map/all_to_all | solution.py:182
  55.1 1.0 copy-start.25
  55.1 1.0 copy-start.27
  69.9 1.6 copy-start.34
  71.3 0.9 copy-start.33
  71.5 15.6 %copy-start.28 = (bf16[2,512,4,128]{3,1,2,0:T(8,128)(2,1)}, bf16[2,512,4,128]{3,1,2,0:T(8,128)(2,1)S(1)}, u32[]{:S(2)}) copy-start(bf16[2,512,4,128]{3,1,2,0:T(8,128)(2,1)S(1)} %bitcast_select_fusion) | copy-start | bytes 3145732
  74.8 1.2 copy-start.2
  74.8 1.6 copy-start.22
  74.8 1.9 copy-start.23
  82.7 1.2 copy-start.4
  82.7 1.2 copy-start.7
  82.7 1.2 copy-start.9
  83.3 1.2 copy-start.1
  83.3 1.5 copy-start.19
  83.3 2.0 copy-start.21
  84.0 1.9 copy-start.6
  87.1 0.8 copy-start.42
  87.2 2.3 %copy-start.44 = (f32[512]{0:T(512)}, f32[512]{0:T(512)S(1)}, u32[]{:S(2)}) copy-start(f32[512]{0:T(512)S(1)} %get-tuple-element.10) | copy-start | bytes 6148
  88.9 0.9 copy-start.13
  88.9 1.0 copy-start.15
  88.9 1.3 copy-start.11
  89.9 1.9 copy-start.17
  93.0 6.7 %copy-start.45 = (f32[512]{0:T(512)S(1)}, f32[512]{0:T(512)}, u32[]{:S(2)}) copy-start(f32[512]{0:T(512)} %copy-done.44) | copy-start | bytes 6148
  95.4 19.6 %all-to-all-start.4 = ((bf16[2,512,4,128]{3,2,0,1:T(4,128)(2,1)}), bf16[2,512,4,128]{3,2,0,1:T(4,128)(2,1)}, u32[]{:S(2)}, u32[]{:S(2)}) async-start(bf16[2,512,4,128]{3,2,0,1:T(4,128)(2,1)} %copy.68), calls=%async_computation.4 | async-start | bytes 2097152 | tf_op jit(solution)/shard_map/all_to_all | solution.py:242
  99.7 1.7 copy-start.20
  99.7 1.7 copy-start.43
  101.4 1.4 copy-start.36
  101.4 1.4 copy-start.37
  101.4 1.4 copy-start.38
  101.4 1.4 copy-start.39
  101.4 1.4 copy-start.40
  102.9 1.3 copy-start.10
  103.0 2.2 %copy-start.8 = (bf16[512,512]{0,1:T(8,128)(2,1)S(1)}, bf16[512,512]{0,1:T(8,128)(2,1)}, u32[]{:S(2)}) copy-start(bf16[512,512]{0,1:T(8,128)(2,1)} %copy-done.7) | copy-start | bytes 1572868
  115.1 26.4 %all-to-all-start.6 = ((bf16[2,512,1,128]{3,0,2,1:T(2,128)(2,1)}), bf16[2,512,1,128]{3,0,2,1:T(2,128)(2,1)S(1)}, u32[]{:S(2)}, u32[]{:S(2)}) async-start(bf16[2,512,1,128]{3,0,2,1:T(2,128)(2,1)} %copy.74), calls=%async_computation.6 | async-start | bytes 524288 | tf_op jit(solution)/shard_map/all_to_all | solution.py:244
  118.5 52.1 %reduce-scatter.2.cloned.1.call-start = ((), (), s32[]{:S(2)}) async-start(), calls=%async_computation.8 | async-start | bytes 1179648 | tf_op jit(solution)/shard_map/reduce_scatter | solution.py:259
  132.8 1.5 copy-start.16
  134.3 1.0 copy-start.14
  135.4 1.0 copy-start.12
  136.4 1.0 copy-start.18
  137.4 1.0 copy-start.5
  137.4 1.4 copy-start.32
  137.5 2.0 copy-start.31
  141.4 32.7 %copy-start.3 = (bf16[2,64,8,4,128]{4,3,2,1,0:T(4,128)(2,1)S(1)}, bf16[2,64,8,4,128]{4,3,2,1,0:T(4,128)(2,1)}, u32[]{:S(2)}) copy-start(bf16[2,64,8,4,128]{4,3,2,1,0:T(4,128)(2,1)} %copy.70) | copy-start | bytes 3145732
  141.5 31.7 %all-to-all-start.5 = ((bf16[2,512,1,128]{3,0,2,1:T(2,128)(2,1)}), bf16[2,512,1,128]{3,0,2,1:T(2,128)(2,1)S(1)}, u32[]{:S(2)}, u32[]{:S(2)}) async-start(bf16[2,512,1,128]{3,0,2,1:T(2,128)(2,1)} %copy.71), calls=%async_computation.5 | async-start | bytes 524288 | tf_op jit(solution)/shard_map/all_to_all | solution.py:243
  145.7 62.5 %all-reduce.3.cloned.1.call-start = ((), (), s32[]{:S(2)}) async-start(), calls=%async_computation.9 | async-start | bytes 262144 | tf_op jit(solution)/shard_map/psum | solution.py:274
Sparse Core Ops, SparseCore 0:
  132.9 37.5 reduce-scatter.1
  173.5 34.6 all-reduce.2
where the time goes:
time: 219 us; the launch traced here: 218 us
  waiting for transfers between devices  91.6 us (42%)
  matrix products  35.7 us (16%)
  local copies, waits for them, and re-layouts  30 us (14%)
  starting transfers between devices  28.5 us (13%)
  other arithmetic  17.3 us (8%)
  between operations  14.9 us (7%)
    dot_general x34, matrix products, contract_axes(): lax.dot_general(first_operand, second_operand, (((first_axis,), (second_a...  33.6 us
    psum x1, waiting for transfers between devices, on_device(): lax.psum(down_local.astype(jnp.bfloat16), 'dp').astype(jnp.float32)  32.4 us
    reduce_scatter x1, waiting for transfers between devices, on_device(): lax.psum_scatter(jnp.concatenate([contract_axes(hidden_state, backward_gr...  24.8 us
    all_to_all x1, waiting for transfers between devices, on_device(): lax.all_to_all(query_tokens, 'seq', split_axis=2, concat_axis=1, tiled=True)  13.4 us
    all_to_all x1, waiting for transfers between devices, on_device(): lax.all_to_all(query_back, 'seq', split_axis=1, concat_axis=2, tiled=True)  8.72 us
    all_to_all x1, waiting for transfers between devices, on_device(): lax.all_to_all(value_arranged, 'seq', split_axis=2, concat_axis=1, tiled=...  6.08 us
    unnamed x94, local copies, waits for them, and re-layouts  5.95 us
    all_to_all x1, starting transfers between devices, on_device(): lax.all_to_all(key_arranged, 'seq', split_axis=2, concat_axis=1, tiled=True)  5.2 us
  transfers between devices with their start and end apart: 9, of which 7 were waited for; matrix products, arithmetic and copies ran while one was open for 23% of the time, Pallas kernels for 0%

commit v1 on v0

--- a/solution.py
+++ b/solution.py
@@ -3,6 +3,8 @@
 import jax
 import jax.numpy as jnp
 from jax import lax
+from jax.experimental import pallas as pl
+from jax.experimental.pallas import tpu as pltpu
 from jax.sharding import PartitionSpec as P
 
 HEAD_WIDTH = 128
@@ -283,6 +285,415 @@
     )
 
 
+CHUNKS = 4
+VMEM_BUDGET = 44 * 1024 * 1024
+NEG = -1e30
+
+
+def nt_dot(left, right):
+    return lax.dot_general(
+        left, right, (((1,), (1,)), ((), ())), preferred_element_type=jnp.float32
+    )
+
+
+def subsets(bits):
+    masks = [0]
+    for bit in bits:
+        masks = masks + [mask | (1 << bit) for mask in masks]
+    return masks
+
+
+def fused_kernel(
+    n_seq,
+    n_dp,
+    n_roll,
+    tokens,
+    kv_heads,
+    group,
+    rank,
+    chunks,
+    off_ref,
+    len_ref,
+    cos_ref,
+    sin_ref,
+    q_ref,
+    k_ref,
+    v_ref,
+    g_ref,
+    hid_ref,
+    down_ref,
+    up_ref,
+    gq_ref,
+    gk_ref,
+    gv_ref,
+    gd_ref,
+    gu_ref,
+    kv_all,
+    dkv,
+    red_buf,
+    ad_buf,
+    ad_red,
+    dp_buf,
+    ag_send,
+    ag_recv,
+    rs_send,
+    rs_recv,
+    ad_send,
+    ad_recv,
+    dp_send,
+    dp_recv,
+):
+    me = lax.axis_index("seq")
+    my_dp = lax.axis_index("dp")
+    n_bits = n_seq.bit_length() - 1
+    chip_bits = list(range(1, n_bits))
+    gather_orders = [chip_bits + [0], chip_bits[::-1] + [0]]
+    reduce_orders = [[0] + chip_bits[::-1], [0] + chip_bits]
+    heads_per = kv_heads // chunks
+    width = HEAD_WIDTH
+    rows = group * tokens
+    length = n_seq * tokens
+    scale = width ** (-0.5)
+    cols = q_ref.shape[1] // n_seq
+    pending = []
+
+    barrier = pltpu.get_barrier_semaphore()
+    for bit in range(n_bits):
+        pl.semaphore_signal(barrier, inc=1, device_id={"seq": me ^ (1 << bit)})
+    for step in range(1, n_dp):
+        pl.semaphore_signal(barrier, inc=1, device_id={"dp": lax.rem(my_dp + step, n_dp)})
+
+    cos = cos_ref[...]
+    sin = sin_ref[...]
+
+    def slot_rows(mask):
+        return pl.ds(pl.multiple_of((me ^ mask) * tokens, tokens), tokens)
+
+    def load_chunk(c):
+        for h in range(c * heads_per, (c + 1) * heads_per):
+            for r in range(n_roll):
+                span = slice(r * tokens, (r + 1) * tokens)
+                lane = slice(h * width, (h + 1) * width)
+                key = k_ref[span, lane].astype(jnp.float32)
+                key = key * cos + pltpu.roll(key, width // 2, 1) * sin
+                kv_all[0, h, r, slot_rows(0), :] = key.astype(jnp.bfloat16)
+                kv_all[1, h, r, slot_rows(0), :] = v_ref[span, lane]
+
+    gather_ops = {}
+
+    def gather_send(c, stage):
+        for t in range(2):
+            order = gather_orders[t]
+            bit = order[stage]
+            for mask in subsets(order[:stage]):
+                block = kv_all.at[
+                    t, pl.ds(c * heads_per, heads_per), slice(None), slot_rows(mask), slice(None)
+                ]
+                got = mask | (1 << bit)
+                copy = pltpu.make_async_remote_copy(
+                    src_ref=block,
+                    dst_ref=block,
+                    send_sem=ag_send.at[t, c, got],
+                    recv_sem=ag_recv.at[t, c, got],
+                    device_id={"seq": me ^ (1 << bit)},
+                )
+                copy.start()
+                gather_ops.setdefault((c, stage), []).append(copy)
+                pending.append(copy)
+
+    def gather_wait(c, stage):
+        for copy in gather_ops[(c, stage)]:
+            copy.wait_recv()
+
+    reduce_ops = {}
+
+    def reduce_send(c, stage):
+        for t in range(2):
+            order = reduce_orders[t]
+            bit = order[stage]
+            for rest in subsets(order[stage + 1 :]):
+                mask = rest | (1 << bit)
+                head_span = pl.ds(c * heads_per, heads_per)
+                copy = pltpu.make_async_remote_copy(
+                    src_ref=dkv.at[t, head_span, slice(None), slot_rows(mask), slice(None)],
+                    dst_ref=red_buf.at[t, mask, head_span],
+                    send_sem=rs_send.at[t, c, mask],
+                    recv_sem=rs_recv.at[t, c, mask],
+                    device_id={"seq": me ^ (1 << bit)},
+                )
+                copy.start()
+                reduce_ops.setdefault((c, stage), []).append((t, mask, rest, copy))
+                pending.append(copy)
+
+    def reduce_add(c, stage):
+        for t, mask, rest, copy in reduce_ops[(c, stage)]:
+            copy.wait_recv()
+            for h in range(c * heads_per, (c + 1) * heads_per):
+                for r in range(n_roll):
+                    total = dkv[t, h, r, slot_rows(rest), :].astype(jnp.float32)
+                    total = total + red_buf[t, mask, h, r].astype(jnp.float32)
+                    if stage < n_bits - 1:
+                        dkv[t, h, r, slot_rows(rest), :] = total.astype(jnp.bfloat16)
+                        continue
+                    span = slice(r * tokens, (r + 1) * tokens)
+                    lane = slice(h * width, (h + 1) * width)
+                    if t == 0:
+                        total = total * cos - pltpu.roll(total, width // 2, 1) * sin
+                        gk_ref[span, lane] = total.astype(jnp.bfloat16)
+                    else:
+                        gv_ref[span, lane] = total.astype(jnp.bfloat16)
+
+    def advance_reduce(c, stage):
+        if stage > 0:
+            reduce_add(c, stage - 1)
+        if stage < n_bits:
+            reduce_send(c, stage)
+
+    adapter_ops = {}
+
+    def adapter_send(stage):
+        for t in range(2):
+            order = reduce_orders[t]
+            bit = order[stage]
+            for rest in subsets(order[stage + 1 :]):
+                mask = rest | (1 << bit)
+                copy = pltpu.make_async_remote_copy(
+                    src_ref=ad_buf.at[t, me ^ mask],
+                    dst_ref=ad_red.at[t, mask],
+                    send_sem=ad_send.at[t, mask],
+                    recv_sem=ad_recv.at[t, mask],
+                    device_id={"seq": me ^ (1 << bit)},
+                )
+                copy.start()
+                adapter_ops.setdefault(stage, []).append((t, mask, rest, copy))
+                pending.append(copy)
+
+    def adapter_add(stage):
+        for t, mask, rest, copy in adapter_ops[stage]:
+            copy.wait_recv()
+            total = ad_buf[t, me ^ rest].astype(jnp.float32) + ad_red[t, mask].astype(jnp.float32)
+            total = total.astype(jnp.bfloat16)
+            if stage < n_bits - 1:
+                ad_buf[t, me ^ rest] = total
+            else:
+                dp_buf[my_dp, t] = total
+
+    def advance_adapter(stage):
+        if stage > 0:
+            adapter_add(stage - 1)
+        if stage < n_bits:
+            adapter_send(stage)
+
+    key_index = lax.broadcasted_iota(jnp.int32, (length, rows), 0)
+    row_index = me * tokens + lax.broadcasted_iota(jnp.int32, (1, rows), 1) % tokens
+    token_index = me * tokens + lax.broadcasted_iota(jnp.int32, (tokens, width), 0)
+
+    def pair_work(c, index):
+        h = c * heads_per + index // n_roll
+        r = index % n_roll
+        span = pl.ds(pl.multiple_of(r * tokens, tokens), tokens)
+        offset = off_ref[r]
+        keep = (token_index >= offset) & (token_index < len_ref[r])
+        queries = []
+        grads = []
+        for j in range(group):
+            lane = pl.ds(pl.multiple_of((h * group + j) * width, width), width)
+            query = q_ref[span, lane].astype(jnp.float32)
+            query = query * cos + pltpu.roll(query, width // 2, 1) * sin
+            queries.append(query.astype(jnp.bfloat16))
+            grad = g_ref[span, lane].astype(jnp.float32)
+            grads.append(jnp.where(keep, grad, 0.0).astype(jnp.bfloat16))
+        query = jnp.concatenate(queries, axis=0)
+        grad = jnp.concatenate(grads, axis=0)
+        key = kv_all[0, h, r]
+        value = kv_all[1, h, r]
+        visible = (key_index == row_index) | ((key_index >= offset) & (key_index <= row_index))
+        scores = jnp.where(visible, nt_dot(key, query) * scale, NEG)
+        weights = jnp.exp(scores - jnp.max(scores, axis=0, keepdims=True))
+        prob = weights * (1.0 / jnp.sum(weights, axis=0, keepdims=True))
+        grad_prob = nt_dot(value, grad)
+        delta = jnp.sum(prob * grad_prob, axis=0, keepdims=True)
+        grad_score = (prob * (grad_prob - delta) * scale).astype(jnp.bfloat16)
+        prob_low = prob.astype(jnp.bfloat16)
+        dkv[1, h, r] = jnp.dot(prob_low, grad, preferred_element_type=jnp.float32).astype(
+            jnp.bfloat16
+        )
+        dkv[0, h, r] = jnp.dot(grad_score, query, preferred_element_type=jnp.float32).astype(
+            jnp.bfloat16
+        )
+        back = jnp.dot(key.T, grad_score, preferred_element_type=jnp.float32).T
+        for j in range(group):
+            lane = pl.ds(pl.multiple_of((h * group + j) * width, width), width)
+            part = back[j * tokens : (j + 1) * tokens]
+            part = part * cos - pltpu.roll(part, width // 2, 1) * sin
+            gq_ref[span, lane] = part.astype(jnp.bfloat16)
+
+    def compute_chunk(c):
+        def body(index, carry):
+            pair_work(c, index)
+            return carry
+
+        lax.fori_loop(0, heads_per * n_roll, body, 0)
+
+    load_chunk(0)
+    pl.semaphore_wait(barrier, n_bits + n_dp - 1)
+    latent = None
+    for slot in range(chunks + 2 * n_bits + 1):
+        for c in range(chunks):
+            stage = slot - c
+            if stage == 0 and c > 0:
+                load_chunk(c)
+            if 0 < stage <= n_bits:
+                gather_wait(c, stage - 1)
+            if 0 <= stage < n_bits:
+                gather_send(c, stage)
+        for c in range(chunks):
+            stage = slot - c - n_bits
+            if 1 <= stage <= n_bits:
+                advance_reduce(c, stage)
+        if slot == 0:
+            latent = (
+                jnp.dot(hid_ref[...], down_ref[...], preferred_element_type=jnp.float32)
+                .T.astype(jnp.bfloat16)
+            )
+        ready = slot - n_bits
+        if 0 <= ready < chunks:
+            compute_chunk(ready)
+            advance_reduce(ready, 0)
+        if ready == chunks - 1:
+            back = nt_dot(up_ref[...], gq_ref[...]).astype(jnp.bfloat16)
+            for d in range(n_seq):
+                lane = slice(d * cols, (d + 1) * cols)
+                ad_buf[0, d] = jnp.dot(
+                    back, hid_ref[:, lane], preferred_element_type=jnp.float32
+                ).astype(jnp.bfloat16)
+                ad_buf[1, d] = jnp.dot(
+                    latent, gq_ref[:, lane], preferred_element_type=jnp.float32
+                ).astype(jnp.bfloat16)
+            advance_adapter(0)
+        elif chunks <= ready < chunks + n_bits:
+            advance_adapter(ready - chunks + 1)
+
+    dp_ops = []
+    for step in range(1, n_dp):
+        copy = pltpu.make_async_remote_copy(
+            src_ref=dp_buf.at[my_dp],
+            dst_ref=dp_buf.at[my_dp],
+            send_sem=dp_send.at[step],
+            recv_sem=dp_recv.at[step],
+            device_id={"dp": lax.rem(my_dp + step, n_dp)},
+        )
+        copy.start()
+        dp_ops.append(copy)
+        pending.append(copy)
+    for copy in dp_ops:
+        copy.wait_recv()
+    down_total = dp_buf[0, 0].astype(jnp.float32)
+    up_total = dp_buf[0, 1].astype(jnp.float32)
+    for d in range(1, n_dp):
+        down_total = down_total + dp_buf[d, 0].astype(jnp.float32)
+        up_total = up_total + dp_buf[d, 1].astype(jnp.float32)
+    gd_ref[...] = down_total.T
+    gu_ref[...] = up_total
+    for copy in pending:
+        copy.wait_send()
+
+
+def fused_on_device(
+    n_seq,
+    n_dp,
+    queries,
+    unrotated_key_rows,
+    value_projection_rows,
+    attention_output_gradient,
+    normed_hidden_input,
+    adapter_down_weight,
+    adapter_up_weight,
+    lengths,
+    offsets,
+):
+    n_roll, tokens, q_width = queries.shape
+    kv_width = unrotated_key_rows.shape[2]
+    kv_heads = kv_width // HEAD_WIDTH
+    group = q_width // kv_width
+    rank = adapter_down_weight.shape[1]
+    chunks = min(CHUNKS, kv_heads)
+    flat = n_roll * tokens
+    half = HEAD_WIDTH // 2
+    frequency = rotary_base ** (-(jnp.arange(half, dtype=jnp.float32) * 2.0 / HEAD_WIDTH))
+    positions = lax.axis_index("seq") * tokens + jnp.arange(tokens, dtype=jnp.int32)
+    angles = positions.astype(jnp.float32)[:, None] * frequency[None, :]
+    cosine, sine = jnp.cos(angles), jnp.sin(angles)
+    cos_wide = jnp.concatenate([cosine, cosine], axis=1)
+    sin_wide = jnp.concatenate([-sine, sine], axis=1)
+    vmem = pl.BlockSpec(memory_space=pltpu.VMEM)
+    smem = pl.BlockSpec(memory_space=pltpu.SMEM)
+    cols = q_width // n_seq
+    low = jnp.bfloat16
+    dma = pltpu.SemaphoreType.DMA
+    outs = pl.pallas_call(
+        partial(fused_kernel, n_seq, n_dp, n_roll, tokens, kv_heads, group, rank, chunks),
+        out_shape=(
+            jax.ShapeDtypeStruct((flat, q_width), low),
+            jax.ShapeDtypeStruct((flat, kv_width), low),
+            jax.ShapeDtypeStruct((flat, kv_width), low),
+            jax.ShapeDtypeStruct((cols, rank), jnp.float32),
+            jax.ShapeDtypeStruct((rank, cols), jnp.float32),
+        ),
+        in_specs=[smem, smem] + [vmem] * 9,
+        out_specs=[vmem] * 5,
+        scratch_shapes=[
+            pltpu.VMEM((2, kv_heads, n_roll, n_seq * tokens, HEAD_WIDTH), low),
+            pltpu.VMEM((2, kv_heads, n_roll, n_seq * tokens, HEAD_WIDTH), low),
+            pltpu.VMEM((2, n_seq, kv_heads, n_roll, tokens, HEAD_WIDTH), low),
+            pltpu.VMEM((2, n_seq, rank, cols), low),
+            pltpu.VMEM((2, n_seq, rank, cols), low),
+            pltpu.VMEM((n_dp, 2, rank, cols), low),
+            dma((2, chunks, n_seq)),
+            dma((2, chunks, n_seq)),
+            dma((2, chunks, n_seq)),
+            dma((2, chunks, n_seq)),
+            dma((2, n_seq)),
+            dma((2, n_seq)),
+            dma((n_dp,)),
+            dma((n_dp,)),
+        ],
+        compiler_params=pltpu.CompilerParams(
+            collective_id=0, has_side_effects=True, vmem_limit_bytes=60 * 1024 * 1024
+        ),
+    )(
+        offsets,
+        lengths,
+        cos_wide,
+        sin_wide,
+        queries.reshape(flat, q_width),
+        unrotated_key_rows.reshape(flat, kv_width),
+        value_projection_rows.reshape(flat, kv_width),
+        attention_output_gradient.reshape(flat, q_width),
+        normed_hidden_input.reshape(flat, q_width),
+        adapter_down_weight,
+        adapter_up_weight,
+    )
+    grad_query, grad_key, grad_value, grad_down, grad_up = outs
+    return (
+        grad_query.reshape(n_roll, tokens, q_width),
+        grad_key.reshape(n_roll, tokens, kv_width),
+        grad_value.reshape(n_roll, tokens, kv_width),
+        grad_down,
+        grad_up,
+    )
+
+
+def dispatch(mesh, *args):
+    n_seq = mesh.shape["seq"]
+    n_roll, tokens, q_width = args[0].shape
+    kv_width = args[1].shape[2]
+    gathered = 2 * n_roll * n_seq * tokens * kv_width * 2
+    if 3 * gathered + 7 * n_roll * tokens * q_width * 2 > VMEM_BUDGET:
+        return on_device(*args)
+    return fused_on_device(n_seq, mesh.shape["dp"], *args)
+
+
 def solution(mesh):
     in_specs = (
         P("dp", "seq", None),
@@ -303,5 +714,5 @@
         P(None, "seq"),
     )
     return jax.shard_map(
-        on_device, mesh=mesh, in_specs=in_specs, out_specs=out_specs, check_vma=False
-    )
+        partial(dispatch, mesh), mesh=mesh, in_specs=in_specs, out_specs=out_specs, check_vma=False
+    )

time: 219 us -> 85.1 us (0.39)
  waiting for transfers between devices: 91.6 us -> 0 us
  Pallas kernels: 0 us -> 74.2 us
  matrix products: 35.7 us -> 0 us
  starting transfers between devices: 28.5 us -> 0 us
  local copies, waits for them, and re-layouts: 30 us -> 9.11 us
  other arithmetic: 17.3 us -> 0.93 us
  between operations: 14.9 us -> 0.67 us
    pallas_call x0 -> x1, Pallas kernels: none -> 74.2 us  [fused_on_device(): pl.pallas_call(partial(fused_kernel, n_seq, n_dp, n_roll, tokens, kv_head...]
    dot_general x42 -> x0, matrix products: 35.7 us -> none  [the longest x34 33.6 us: contract_axes(): lax.dot_general(first_operand, second_operand, (((first_axis,), (second_a...]
    all_to_all x7 -> x0, waiting for transfers between devices: 34.3 us -> none  [the longest x1 13.4 us: on_device(): lax.all_to_all(query_tokens, 'seq', split_axis=2, concat_axis=1, tiled=True)]
    psum x1 -> x0, waiting for transfers between devices: 32.4 us -> none  [on_device(): lax.psum(down_local.astype(jnp.bfloat16), 'dp').astype(jnp.float32)]
    all_to_all x7 -> x0, starting transfers between devices: 28.5 us -> none  [the longest x1 5.2 us: on_device(): lax.all_to_all(key_arranged, 'seq', split_axis=2, concat_axis=1, tiled=True)]
    reduce_scatter x1 -> x0, waiting for transfers between devices: 24.8 us -> none  [on_device(): lax.psum_scatter(jnp.concatenate([contract_axes(hidden_state, backward_gr...]
    another operation x6 -> x0, local copies, waits for them, and re-layouts: 8.29 us -> none  [the longest x2 2.64 us: arrange_rows(): jnp.transpose(split, (0, 2, 3, 1, 4))]
    reshape x3 -> x0, local copies, waits for them, and re-layouts: 5.14 us -> none  [the longest x1 2.6 us: on_device(): flattened_query = query_result.reshape(rollout_count * tokens, query_width)]
  transfers between devices with their start and end apart: 9 -> 0, of which waited for: 7 -> 0; matrix products, arithmetic and copies ran while one was open for 23% -> 0% of each run, Pallas kernels for 0% -> 0%
where the time goes in v1:
time: 85.1 us; the launch traced here: 84.9 us
  Pallas kernels  74.2 us (87%)
  local copies, waits for them, and re-layouts  9.11 us (11%)
  other arithmetic  0.93 us (1%)
    pallas_call x1, Pallas kernels, fused_on_device(): pl.pallas_call(partial(fused_kernel, n_seq, n_dp, n_roll, tokens, kv_head...  74.2 us
    unnamed x12, local copies, waits for them, and re-layouts  9.11 us

profile of v1, /device:TPU:0, one launch (start us, length us, event | category | flops | bytes accessed | tf_op | source)
XLA Modules:
  0.0 84.9 jit_solution(14463787613636720400)
XLA Ops:
  0.7 0.2 fusion
  0.9 0.7 pad_maximum_fusion
  1.6 2.4 %copy.14.down_ref = bf16[4096,64]{1,0:T(8,128)(2,1)} copy(bf16[4096,64]{0,1:T(8,128)(2,1)} %param.14) | data formatting | bytes 1048576 | tf_op args[5]
  3.9 74.2 %shard_map.128 = (bf16[128,4096]{1,0:T(8,128)(2,1)}, bf16[128,1024]{1,0:T(8,128)(2,1)}, bf16[128,1024]{1,0:T(8,128)(2,1)}, f32[512,64]{1,0:T(8,128)}, f32[64,512]{1,0:T(8,128)}) custom-call(s32[2]{0:T(128)} %off_ref.1, s32[2]{0:T(128)} %len_ref.1, f32[64,128]{1,0:T(8,128)} %get-tuple-element.23.cos_ref, f32[64,128]{1,0:T(8,128)} %get-tuple-element.24.sin_ref, ...), custom_call_target="tpu_custom_call" | custom-call | tf_op jit(solution)/shard_map/pallas_call | solution.py:634
  78.1 1.7 %copy.15 = f32[512,64]{0,1:T(8,128)} copy(f32[512,64]{1,0:T(8,128)} %get-tuple-element.18) | data formatting | bytes 262144
  79.8 0.0 copy-start.1
  79.8 2.3 %copy.20 = bf16[2,64,4096]{2,1,0:T(8,128)(2,1)} copy(bf16[2,64,4096]{2,1,0:T(8,128)(2,1)} %bitcast.8) | data formatting | bytes 2097152
  82.2 0.0 copy-done.1
  82.2 0.0 copy-start
  82.2 0.7 copy.21
  82.9 0.3 copy-done
  83.2 0.0 copy-start.2
  83.2 0.7 copy.22
  83.9 0.3 copy-done.2
  84.2 0.7 copy.23
  (2 shorter events, 0.0 us)
Async XLA Ops:
  79.8 2.3 %copy-start.1 = (bf16[128,1024]{1,0:T(8,128)(2,1)S(1)}, bf16[128,1024]{1,0:T(8,128)(2,1)}, u32[]{:S(2)}) copy-start(bf16[128,1024]{1,0:T(8,128)(2,1)} %get-tuple-element.11) | copy-start | bytes 786436
  82.2 1.0 %copy-start = (bf16[128,1024]{1,0:T(8,128)(2,1)S(1)}, bf16[128,1024]{1,0:T(8,128)(2,1)}, u32[]{:S(2)}) copy-start(bf16[128,1024]{1,0:T(8,128)(2,1)} %get-tuple-element.12) | copy-start | bytes 786436
  83.2 1.0 %copy-start.2 = (f32[64,512]{1,0:T(8,128)S(1)}, f32[64,512]{1,0:T(8,128)}, u32[]{:S(2)}) copy-start(f32[64,512]{1,0:T(8,128)} %get-tuple-element.34) | copy-start | bytes 393220

commit v2 on v1

--- a/solution.py
+++ b/solution.py
@@ -552,10 +552,7 @@
             if 1 <= stage <= n_bits:
                 advance_reduce(c, stage)
         if slot == 0:
-            latent = (
-                jnp.dot(hid_ref[...], down_ref[...], preferred_element_type=jnp.float32)
-                .T.astype(jnp.bfloat16)
-            )
+            latent = nt_dot(down_ref[...], hid_ref[...]).astype(jnp.bfloat16)
         ready = slot - n_bits
         if 0 <= ready < chunks:
             compute_chunk(ready)
@@ -593,7 +590,7 @@
     for d in range(1, n_dp):
         down_total = down_total + dp_buf[d, 0].astype(jnp.float32)
         up_total = up_total + dp_buf[d, 1].astype(jnp.float32)
-    gd_ref[...] = down_total.T
+    gd_ref[...] = down_total
     gu_ref[...] = up_total
     for copy in pending:
         copy.wait_send()
@@ -637,7 +634,7 @@
             jax.ShapeDtypeStruct((flat, q_width), low),
             jax.ShapeDtypeStruct((flat, kv_width), low),
             jax.ShapeDtypeStruct((flat, kv_width), low),
-            jax.ShapeDtypeStruct((cols, rank), jnp.float32),
+            jax.ShapeDtypeStruct((rank, cols), jnp.float32),
             jax.ShapeDtypeStruct((rank, cols), jnp.float32),
         ),
         in_specs=[smem, smem] + [vmem] * 9,
@@ -671,7 +668,7 @@
         value_projection_rows.reshape(flat, kv_width),
         attention_output_gradient.reshape(flat, q_width),
         normed_hidden_input.reshape(flat, q_width),
-        adapter_down_weight,
+        adapter_down_weight.T,
         adapter_up_weight,
     )
     grad_query, grad_key, grad_value, grad_down, grad_up = outs
@@ -679,7 +676,7 @@
         grad_query.reshape(n_roll, tokens, q_width),
         grad_key.reshape(n_roll, tokens, kv_width),
         grad_value.reshape(n_roll, tokens, kv_width),
-        grad_down,
+        grad_down.T,
         grad_up,
     )
 

time: 85.1 us -> 81.7 us (0.960)
  local copies, waits for them, and re-layouts: 9.11 us -> 5.98 us
    unnamed x12 -> x13, local copies, waits for them, and re-layouts: 9.11 us -> 5.98 us
where the time goes in v2:
time: 81.7 us; the launch traced here: 81.4 us
  Pallas kernels  73.9 us (90%)
  local copies, waits for them, and re-layouts  5.98 us (7%)
  other arithmetic  0.93 us (1%)
    pallas_call x1, Pallas kernels, fused_on_device(): pl.pallas_call(partial(fused_kernel, n_seq, n_dp, n_roll, tokens, kv_head...  73.9 us
    unnamed x13, local copies, waits for them, and re-layouts  5.98 us

profile of v2, /device:TPU:0, one launch (start us, length us, event | category | flops | bytes accessed | tf_op | source)
XLA Modules:
  0.0 81.4 jit_solution(11942308575766145727)
XLA Ops:
  0.7 0.2 fusion
  0.9 0.7 pad_maximum_fusion
  1.6 73.9 %shard_map.128 = (bf16[128,4096]{1,0:T(8,128)(2,1)}, bf16[128,1024]{1,0:T(8,128)(2,1)}, bf16[128,1024]{1,0:T(8,128)(2,1)}, f32[64,512]{1,0:T(8,128)}, f32[64,512]{1,0:T(8,128)}) custom-call(s32[2]{0:T(128)} %off_ref.1, s32[2]{0:T(128)} %len_ref.1, f32[64,128]{1,0:T(8,128)} %get-tuple-element.18.cos_ref, f32[64,128]{1,0:T(8,128)} %get-tuple-element.19.sin_ref, ...), custom_call_target="tpu_custom_call" | custom-call | tf_op jit(solution)/shard_map/pallas_call | solution.py:631
  75.4 0.0 copy-start.1
  75.5 2.3 %copy.19 = bf16[2,64,4096]{2,1,0:T(8,128)(2,1)} copy(bf16[2,64,4096]{2,1,0:T(8,128)(2,1)} %bitcast.10) | data formatting | bytes 2097152
  77.8 0.0 copy-done.1
  77.8 0.0 copy-start
  77.8 0.7 copy.20
  78.5 0.3 copy-done
  78.8 0.0 copy-start.3
  78.8 0.7 copy.21
  79.5 0.3 copy-done.3
  79.8 0.0 copy-start.2
  79.8 0.7 copy.22
  80.5 0.3 copy-done.2
  80.8 0.7 copy.23
  (2 shorter events, 0.0 us)
Async XLA Ops:
  75.4 2.3 %copy-start.1 = (bf16[128,1024]{1,0:T(8,128)(2,1)S(1)}, bf16[128,1024]{1,0:T(8,128)(2,1)}, u32[]{:S(2)}) copy-start(bf16[128,1024]{1,0:T(8,128)(2,1)} %get-tuple-element.11) | copy-start | bytes 786436
  77.8 1.0 %copy-start = (bf16[128,1024]{1,0:T(8,128)(2,1)S(1)}, bf16[128,1024]{1,0:T(8,128)(2,1)}, u32[]{:S(2)}) copy-start(bf16[128,1024]{1,0:T(8,128)(2,1)} %get-tuple-element.12) | copy-start | bytes 786436
  78.8 1.0 %copy-start.3 = (f32[64,512]{1,0:T(8,128)S(1)}, f32[64,512]{1,0:T(8,128)}, u32[]{:S(2)}) copy-start(f32[64,512]{1,0:T(8,128)} %get-tuple-element.13) | copy-start | bytes 393220
  79.8 1.0 %copy-start.2 = (f32[64,512]{1,0:T(8,128)S(1)}, f32[64,512]{1,0:T(8,128)}, u32[]{:S(2)}) copy-start(f32[64,512]{1,0:T(8,128)} %get-tuple-element.29) | copy-start | bytes 393220
